TPU v7x, 256 devices: a whole 4x4x8 slice. The times are simulated.
256 devices in a mesh: vocab: 64 (over y, z, core), section: 4 (over x).
Axes of the slice: x: 4, y: 4, z: 8, core: 2. Of those that a mesh axis runs over, the one named last changes fastest.
Arguments:
- hidden: bfloat16 [4, 256, 8192], P('section', 'vocab'), may hold values from -64 to 64
- policy_head: bfloat16 [76032, 8192], P(('vocab', 'section')), may hold values from -1 to 1
- reference_head: bfloat16 [76032, 8192], P(('vocab', 'section')), may hold values from -1 to 1
- targets: int32 [4, 256], replicated, may hold values from 0 to 76031
- loss_mask: int32 [4, 256], replicated, may hold values 0 or 1
Outputs:
- token_logprob: float32 [4, 256], replicated
- token_kl: float32 [4, 256], replicated
- totals: float32 [3], replicated
All inputs are finite; a program needn't handle non-finite values.
Results may differ from a plain program's by a relative error of at most 0.0003.
Values may be sent and summed in bfloat16 or wider, within the bound.
No kernel may reach another device: no remote copies, remote signals or barrier semaphores. Data moves between devices by JAX's collectives and lax.ppermute only.
A program may use at most 128 MiB of HBM per device.

v0:
```python
import jax
import jax.numpy as jnp
from jax import lax
from jax.sharding import Mesh
from jax.sharding import PartitionSpec as P

VOCAB_SECTION = ("vocab_0", "vocab_1", "vocab_2", "section")
VOCAB = ("vocab_0", "vocab_1", "vocab_2")


def sent_to_all(array, axis):
    count = lax.axis_size(axis)
    return lax.all_to_all(
        jnp.broadcast_to(array[None], (count, *array.shape)), axis, 0, 0, tiled=True
    )


def laid_out(pieces, dim):
    dims = list(pieces.shape[1:])
    dims[dim] *= pieces.shape[0]
    return jnp.moveaxis(pieces, 0, dim).reshape(dims)


def gather_directly(array, axis, dim):
    pieces = sent_to_all(array, axis)
    return laid_out(pieces, dim)


def all_in_one(array, axis):
    leaves = jax.tree.leaves(array)
    order = sorted(range(len(leaves)), key=lambda k: -leaves[k].size)
    width = (1, *leaves[order[0]].shape)[-1]
    lines = [
        jnp.pad(leaves[k].reshape(-1), (0, -leaves[k].size % width)).reshape(-1, width)
        for k in order
    ]
    both, at, found = (lax.all_gather(jnp.concatenate(lines), axis), 0, {})
    for k, line in zip(order, lines):
        slab = both[:, at : at + len(line)].reshape(len(both), -1)
        found[k] = slab[:, : leaves[k].size].reshape(-1, *leaves[k].shape)
        at += len(line)
    numbers = iter(range(len(leaves)))
    return jax.tree.map(lambda _: found[next(numbers)], array)


def combined_by_axis(array, axes, combine):
    for axis in axes:
        pieces = all_in_one(array, axis)
        array = jax.tree.map(lambda part: part[0], pieces)
        for k in range(1, lax.axis_size(axis)):
            array = combine(array, jax.tree.map(lambda part: part[k], pieces))
    return array


def shard_moments(hidden_rows, wanted, policy_head, reference_head, offset):
    contract_dims = (((1,), (1,)), ((), ()))
    policy_logits = lax.dot_general(
        hidden_rows, policy_head, contract_dims, preferred_element_type=jnp.float32
    )
    refer_logits = lax.dot_general(
        hidden_rows, reference_head, contract_dims, preferred_element_type=jnp.float32
    )
    policy_top = jnp.max(policy_logits, axis=1)
    policy_shift = policy_logits - policy_top[:, None]
    policy_exp = jnp.exp(policy_shift)
    policy_sum = jnp.sum(policy_exp, axis=1)
    policy_first = jnp.sum(policy_exp * policy_shift, axis=1)
    policy_cross = jnp.sum(policy_exp * (policy_logits - refer_logits), axis=1)
    columns = offset + lax.broadcasted_iota(jnp.int32, (1, policy_head.shape[0]), 1)
    chosen = jnp.sum(jnp.where(wanted[:, None] == columns, policy_logits, 0.0), axis=1)
    refer_top = jnp.max(refer_logits, axis=1)
    refer_sum = jnp.sum(jnp.exp(refer_logits - refer_top[:, None]), axis=1)
    return (policy_top, policy_sum, policy_first, policy_cross, chosen, refer_top, refer_sum)


def merge_moments(earlier, later):
    top_one, sum_one, first_one, cross_one, chosen_one, rtop_one, rsum_one = earlier
    top_two, sum_two, first_two, cross_two, chosen_two, rtop_two, rsum_two = later
    policy_top = jnp.maximum(top_one, top_two)
    factor_one = jnp.exp(top_one - policy_top)
    factor_two = jnp.exp(top_two - policy_top)
    policy_sum = factor_one * sum_one + factor_two * sum_two
    policy_first = factor_one * (first_one + (top_one - policy_top) * sum_one) + factor_two * (
        first_two + (top_two - policy_top) * sum_two
    )
    policy_cross = factor_one * cross_one + factor_two * cross_two
    refer_top = jnp.maximum(rtop_one, rtop_two)
    refer_sum = rsum_one * jnp.exp(rtop_one - refer_top) + rsum_two * jnp.exp(rtop_two - refer_top)
    return (
        policy_top,
        policy_sum,
        policy_first,
        policy_cross,
        chosen_one + chosen_two,
        refer_top,
        refer_sum,
    )


def place_moments(moments, shape):
    return tuple((moment.reshape(shape) for moment in moments))


def on_device(hidden, policy_head, reference_head, targets, loss_mask):
    width = hidden.shape[2]
    offset = lax.axis_index(VOCAB_SECTION) * policy_head.shape[0]
    micro_total, token_total = targets.shape
    gathered = gather_directly(hidden, "section", 0)
    portion = lax.all_gather(gathered, VOCAB, axis=1, tiled=True)
    span = portion.shape[1]
    wanted = targets.reshape(-1)
    moments = shard_moments(portion.reshape(-1, width), wanted, policy_head, reference_head, offset)
    moments = place_moments(moments, (micro_total, span))
    local_top, local_sum, local_first, local_cross, local_chosen, local_rtop, local_rsum = moments
    policy_top, policy_sum, policy_first, policy_cross, chosen, refer_top, refer_sum = (
        combined_by_axis(
            (local_top, local_sum, local_first, local_cross, local_chosen, local_rtop, local_rsum),
            VOCAB_SECTION,
            merge_moments,
        )
    )
    policy_lse = policy_top + jnp.log(policy_sum)
    refer_lse = refer_top + jnp.log(refer_sum)
    logprob = chosen - policy_lse
    entropy = jnp.log(policy_sum) - policy_first / policy_sum
    divergence = policy_cross / policy_sum - policy_lse + refer_lse
    weights = loss_mask.astype(jnp.float32)
    scale = 1.0 / (micro_total * token_total)
    totals = (
        jnp.stack(
            [jnp.sum(weights * logprob), jnp.sum(weights * entropy), jnp.sum(weights * divergence)]
        )
        * scale
    )
    return (logprob, divergence, totals)


def solution(mesh):
    torus = Mesh(
        mesh.devices.reshape(4, 8, 2, mesh.shape["section"]),
        ("vocab_0", "vocab_1", "vocab_2", "section"),
    )
    placed = (P("section", VOCAB, None), P(VOCAB_SECTION, None), P(VOCAB_SECTION, None), P(), P())
    return jax.shard_map(
        on_device, mesh=torus, in_specs=placed, out_specs=(P(), P(), P()), check_vma=False
    )
```

profile of v0, /device:TPU:2, one launch (start us, length us, event | category | flops | bytes accessed | tf_op | source)
XLA Modules:
  0.0 223.6 jit_solution(3421117086802259031)
XLA Ops:
  7.2 0.0 copy-start.2
  7.2 0.0 all-gather.11.cloned.1.call-start
  7.2 0.9 broadcast_in_dim.15
  8.1 9.8 %all_to_all.5 = bf16[4,1,4,8192]{3,2,1,0:T(4,128)(2,1)S(1)} all-to-all(bf16[4,1,4,8192]{3,2,1,0:T(4,128)(2,1)S(1)} %broadcast_in_dim.15), channel_id=1, replica_groups=mesh['vocab_0'=4,'vocab_1'=8,'vocab_2'=2,'section'=4] {'section'}, dimensions={0} | all-to-all | bytes 524288 | tf_op jit(solution)/shard_map/all_to_all | solution.py:13
  18.0 0.9 copy.11
  18.9 0.0 all-gather.11.cloned.1.call-update
  18.9 0.0 copy-done.2
  19.0 101.4 %all-gather.11.cloned.1.call-done = bf16[4,1,256,8192]{3,0,1,2:T(4,128)(2,1)} async-done(((bf16[4,1,4,8192]{3,0,1,2:T(4,128)(2,1)}), bf16[4,1,256,8192]{3,0,1,2:T(4,128)(2,1)}) %all-gather.11.cloned.1.call-update) | async-done | bytes 16777232 | tf_op jit(solution)/shard_map/all_gather | solution.py:109
  120.3 14.7 %copy.12 = bf16[4,1,256,8192]{3,2,0,1:T(8,128)(2,1)S(1)} copy(bf16[4,1,256,8192]{3,0,1,2:T(4,128)(2,1)} %all-gather.11.cloned.1.call-done) | data formatting | bytes 33554432 | tf_op jit(solution)/shard_map/all_gather | solution.py:109
  135.0 0.0 copy-start
  135.1 15.1 %fusion.225 = (f32[1024]{0:T(1024)S(1)}, f32[1024,297]{0,1:T(8,128)S(1)}) fusion(bf16[1024,8192]{1,0:T(8,128)(2,1)S(1)} %bitcast.1128, bf16[297,8192]{1,0:T(8,128)(2,1)} %param.6), kind=kOutput, calls=%fused_computation.363 | convolution fusion | flops 4983136256 | bytes 22863872 | tf_op jit(solution)/shard_map/dot_general | solution.py:57
  150.2 0.0 copy-done
  150.2 10.4 %fusion.226 = (f32[1024]{0:T(1024)S(1)}, f32[1024,297]{0,1:T(8,128)S(1)}) fusion(bf16[1024,8192]{1,0:T(8,128)(2,1)} %bitcast.1129, bf16[297,8192]{1,0:T(8,128)(2,1)} %param.7), kind=kOutput, calls=%fused_computation.364 | convolution fusion | flops 4983136256 | bytes 22863872 | tf_op jit(solution)/shard_map/dot_general | solution.py:60
  160.6 0.7 fusion.1
  161.3 0.0 copy-start.1
  161.4 0.1 concatenate.12
  161.4 12.1 %all-gather.5 = f32[4,28,256]{2,1,0:T(8,128)S(1)} all-gather(f32[1,28,256]{2,1,0:T(8,128)S(1)} %bitcast.1130), channel_id=3, replica_groups=mesh['vocab_0'=4,'vocab_1'=8,'vocab_2'=2,'section'=4] {'vocab_0'}, dimensions={0}, use_global_device_ids=true | all-gather | bytes 143360 | tf_op jit(solution)/shard_map/all_gather | solution.py:37
  173.7 0.1 concatenate.13
  173.7 24.9 %all-gather.6 = f32[8,28,256]{2,1,0:T(8,128)S(1)} all-gather(f32[1,28,256]{2,1,0:T(8,128)S(1)} %bitcast.1131), channel_id=4, replica_groups=mesh['vocab_0'=4,'vocab_1'=8,'vocab_2'=2,'section'=4] {'vocab_1'}, dimensions={0}, use_global_device_ids=true | all-gather | bytes 258048 | tf_op jit(solution)/shard_map/all_gather | solution.py:37
  198.7 0.1 fusion.100
  198.8 0.1 concatenate.14
  198.9 1.8 all-gather.7
  200.8 0.1 concatenate.15
  200.9 12.1 %all-gather.8 = f32[4,28,256]{2,1,0:T(8,128)S(1)} all-gather(f32[1,28,256]{2,1,0:T(8,128)S(1)} %bitcast.1133), channel_id=6, replica_groups=mesh['vocab_0'=4,'vocab_1'=8,'vocab_2'=2,'section'=4] {'section'}, dimensions={0}, use_global_device_ids=true | all-gather | bytes 143360 | tf_op jit(solution)/shard_map/all_gather | solution.py:37
  213.0 0.0 copy-done.1
  213.0 1.3 multiply_reduce_fusion.2
  214.3 2.5 %maximum_multiply_fusion = f32[3]{0:T(128)} fusion(f32[1]{0:T(128)} %bitcast.120, f32[1]{0:T(128)} %bitcast.119, f32[1]{0:T(128)} %bitcast.114), kind=kLoop, calls=%fused_computation.362 | loop fusion | flops 9 | bytes 24 | tf_op jit(solution)/shard_map/mul | solution.py:130
  (21 shorter events, 0.3 us)
Async XLA Ops:
  7.2 11.8 %copy-start.2 = (s32[4,256]{1,0:T(4,128)S(1)}, s32[4,256]{1,0:T(4,128)}, u32[]{:S(2)}) copy-start(s32[4,256]{1,0:T(4,128)} %param.8) | copy-start | bytes 12292
  7.2 113.2 %all-gather.11.cloned.1.call-start = ((), (), s32[]{:S(2)}) async-start(), calls=%async_computation.1 | async-start | bytes 17039360 | tf_op jit(solution)/shard_map/all_gather | solution.py:109
  135.0 15.1 %copy-start = (bf16[4,1,256,8192]{3,2,0,1:T(8,128)(2,1)}, bf16[4,1,256,8192]{3,2,0,1:T(8,128)(2,1)S(1)}, u32[]{:S(2)}) copy-start(bf16[4,1,256,8192]{3,2,0,1:T(8,128)(2,1)S(1)} %copy.12) | copy-start | bytes 50331652
  161.3 51.7 %copy-start.1 = (s32[4,256]{1,0:T(4,128)S(1)}, s32[4,256]{1,0:T(4,128)}, u32[]{:S(2)}) copy-start(s32[4,256]{1,0:T(4,128)} %param.9) | copy-start | bytes 12292
Sparse Core Ops, SparseCore 0:
  19.0 101.2 all-gather.10
where the time goes:
time: 224 us
  waiting for transfers between devices  101 us (45%)
  blocking collectives  60.8 us (27%)
  matrix products  25.5 us (11%)
  local copies, waits for them, and re-layouts  16.9 us (8%)
  between operations  14.2 us (6%)
  other arithmetic  4.81 us (2%)
    all_gather x1, waiting for transfers between devices, on_device(): portion = lax.all_gather(gathered, VOCAB, axis=1, tiled=True)  101 us
    all_gather x4, blocking collectives, all_in_one(): both, at, found = (lax.all_gather(jnp.concatenate(lines), axis), 0, {})  50.9 us
    dot_general x1, matrix products, shard_moments(): lax.dot_general(hidden_rows, policy_head, contract_dims, preferred_elemen...  15.1 us
    all_gather x1, local copies, waits for them, and re-layouts, on_device(): portion = lax.all_gather(gathered, VOCAB, axis=1, tiled=True)  14.7 us
    dot_general x1, matrix products, shard_moments(): lax.dot_general(hidden_rows, reference_head, contract_dims, preferred_ele...  10.4 us
    all_to_all x1, blocking collectives, sent_to_all(): lax.all_to_all(jnp.broadcast_to(array[None], (count, *array.shape)), axis...  9.85 us
  transfers between devices with their start and end apart: 1, of which 1 were waited for; matrix products, arithmetic and copies ran while one was open for 0% of the time, Pallas kernels for 0%

commit v1 on v0

--- a/solution.py
+++ b/solution.py
@@ -106,7 +106,9 @@
     offset = lax.axis_index(VOCAB_SECTION) * policy_head.shape[0]
     micro_total, token_total = targets.shape
     gathered = gather_directly(hidden, "section", 0)
-    portion = lax.all_gather(gathered, VOCAB, axis=1, tiled=True)
+    portion = jnp.concatenate(
+        lax.all_to_all(jnp.stack([gathered] * lax.axis_size(VOCAB)), VOCAB, 0, 0), axis=1
+    )
     span = portion.shape[1]
     wanted = targets.reshape(-1)
     moments = shard_moments(portion.reshape(-1, width), wanted, policy_head, reference_head, offset)

time: 224 us -> 511 us (2.28)
  waiting for transfers between devices: 101 us -> 365 us
  local copies, waits for them, and re-layouts: 16.9 us -> 46.2 us
  between operations: 14.2 us -> 0.81 us
  starting transfers between devices: 0.04 us -> 12.5 us
    all_to_all x0 -> x1, waiting for transfers between devices: none -> 365 us  [on_device(): lax.all_to_all(jnp.stack([gathered] * lax.axis_size(VOCAB)), VOCAB, 0, 0)]
    all_gather x1 -> x0, waiting for transfers between devices: 101 us -> none  [on_device(): portion = lax.all_gather(gathered, VOCAB, axis=1, tiled=True)]
    another operation x0 -> x2, local copies, waits for them, and re-layouts: none -> 32.9 us  [the longest x1 23.7 us: on_device(): portion.reshape(-1, width)]
    all_gather x1 -> x0, local copies, waits for them, and re-layouts: 14.7 us -> none  [on_device(): portion = lax.all_gather(gathered, VOCAB, axis=1, tiled=True)]
    all_to_all x0 -> x1, starting transfers between devices: none -> 12.5 us  [on_device(): lax.all_to_all(jnp.stack([gathered] * lax.axis_size(VOCAB)), VOCAB, 0, 0)]
    reshape x0 -> x1, local copies, waits for them, and re-layouts: none -> 11.9 us  [on_device(): jnp.concatenate(lax.all_to_all(jnp.stack([gathered] * lax.axis_size(VOCAB...]
where the time goes in v1:
time: 511 us; the launch traced here: 510 us
  waiting for transfers between devices  365 us (71%)
  blocking collectives  60.4 us (12%)
  local copies, waits for them, and re-layouts  46.2 us (9%)
  matrix products  20.8 us (4%)
  starting transfers between devices  12.5 us (2%)
    all_to_all x1, waiting for transfers between devices, on_device(): lax.all_to_all(jnp.stack([gathered] * lax.axis_size(VOCAB)), VOCAB, 0, 0)  365 us
    all_gather x4, blocking collectives, all_in_one(): both, at, found = (lax.all_gather(jnp.concatenate(lines), axis), 0, {})  50.5 us
    another operation x1, local copies, waits for them, and re-layouts, on_device(): portion.reshape(-1, width)  23.7 us
    all_to_all x1, starting transfers between devices, on_device(): lax.all_to_all(jnp.stack([gathered] * lax.axis_size(VOCAB)), VOCAB, 0, 0)  12.5 us
    reshape x1, local copies, waits for them, and re-layouts, on_device(): jnp.concatenate(lax.all_to_all(jnp.stack([gathered] * lax.axis_size(VOCAB...  11.9 us
    dot_general x1, matrix products, shard_moments(): lax.dot_general(hidden_rows, reference_head, contract_dims, preferred_ele...  10.4 us
    dot_general x1, matrix products, shard_moments(): lax.dot_general(hidden_rows, policy_head, contract_dims, preferred_elemen...  10.4 us
  transfers between devices with their start and end apart: 1, of which 1 were waited for; matrix products, arithmetic and copies ran while one was open for 0% of the time, Pallas kernels for 0%

profile of v1, /device:TPU:2, one launch (start us, length us, event | category | flops | bytes accessed | tf_op | source)
XLA Modules:
  0.0 510.0 jit_solution(8937256547268223433)
XLA Ops:
  0.6 0.9 broadcast_in_dim.15
  1.5 9.8 %all_to_all.10 = bf16[4,1,4,8192]{3,2,1,0:T(4,128)(2,1)S(1)} all-to-all(bf16[4,1,4,8192]{3,2,1,0:T(4,128)(2,1)S(1)} %broadcast_in_dim.15), channel_id=1, replica_groups=mesh['vocab_0'=4,'vocab_1'=8,'vocab_2'=2,'section'=4] {'section'}, dimensions={0} | all-to-all | bytes 524288 | tf_op jit(solution)/shard_map/all_to_all | solution.py:13
  11.4 9.3 %stack.15 = bf16[64,4,4,8192]{3,2,1,0:T(4,128)(2,1)} broadcast(bf16[4,4,8192]{2,1,0:T(4,128)(2,1)S(1)} %bitcast.1129), dimensions={1,2,3} | broadcast | bytes 17039360 | tf_op jit(solution)/shard_map/stack | solution.py:110
  20.7 0.0 copy-start.1
  20.7 12.5 %all-to-all-start.1 = ((bf16[64,4,4,8192]{3,2,1,0:T(4,128)(2,1)}), bf16[64,4,4,8192]{3,2,1,0:T(4,128)(2,1)}, u32[]{:S(2)}, u32[]{:S(2)}) async-start(bf16[64,4,4,8192]{3,2,1,0:T(4,128)(2,1)} %stack.15), calls=%async_computation.1 | async-start | bytes 33554432 | tf_op jit(solution)/shard_map/all_to_all | solution.py:110
  33.2 0.0 copy-done.1
  33.2 364.6 %all-to-all-done.1 = bf16[64,4,4,8192]{3,2,1,0:T(4,128)(2,1)} async-done(((bf16[64,4,4,8192]{3,2,1,0:T(4,128)(2,1)}), bf16[64,4,4,8192]{3,2,1,0:T(4,128)(2,1)}, u32[]{:S(2)}, u32[]{:S(2)}) %all-to-all-start.1) | async-done | bytes 16777248 | tf_op jit(solution)/shard_map/all_to_all | solution.py:110
  397.8 11.9 %copy.8 = bf16[4,64,4,8192]{3,2,1,0:T(4,128)(2,1)} copy(bf16[4,64,4,8192]{3,2,0,1:T(4,128)(2,1)} %bitcast.2) | data formatting | bytes 33554432 | tf_op jit(solution)/shard_map/reshape | solution.py:109
  409.8 23.7 %reshape_reshape.3 = bf16[1024,8192]{1,0:T(8,128)(2,1)} reshape(bf16[4,64,4,8192]{3,2,1,0:T(4,128)(2,1)} %copy.8) | data formatting | bytes 33554432 | tf_op jit(solution)/shard_map/reshape;reshape | solution.py:114
  433.4 10.4 %fusion.225 = (f32[1024]{0:T(1024)S(1)}, f32[1024,297]{0,1:T(8,128)S(1)}) fusion(bf16[1024,8192]{1,0:T(8,128)(2,1)} %reshape_reshape.3, bf16[297,8192]{1,0:T(8,128)(2,1)} %param.6), kind=kOutput, calls=%fused_computation.363 | convolution fusion | flops 4983136256 | bytes 22863872 | tf_op jit(solution)/shard_map/dot_general | solution.py:57
  443.8 10.4 %fusion.226 = (f32[1024]{0:T(1024)S(1)}, f32[1024,297]{0,1:T(8,128)S(1)}) fusion(bf16[1024,8192]{1,0:T(8,128)(2,1)} %reshape_reshape.3, bf16[297,8192]{1,0:T(8,128)(2,1)} %param.7), kind=kOutput, calls=%fused_computation.364 | convolution fusion | flops 4983136256 | bytes 22863872 | tf_op jit(solution)/shard_map/dot_general | solution.py:60
  454.2 0.7 fusion.1
  454.9 0.0 copy-start
  455.0 0.1 concatenate.12
  455.1 12.0 %all-gather.4 = f32[4,28,256]{2,1,0:T(8,128)S(1)} all-gather(f32[1,28,256]{2,1,0:T(8,128)S(1)} %bitcast.1130), channel_id=2, replica_groups=mesh['vocab_0'=4,'vocab_1'=8,'vocab_2'=2,'section'=4] {'vocab_0'}, dimensions={0}, use_global_device_ids=true | all-gather | bytes 143360 | tf_op jit(solution)/shard_map/all_gather | solution.py:37
  467.2 0.1 concatenate.13
  467.3 25.3 %all-gather.5 = f32[8,28,256]{2,1,0:T(8,128)S(1)} all-gather(f32[1,28,256]{2,1,0:T(8,128)S(1)} %bitcast.1131), channel_id=3, replica_groups=mesh['vocab_0'=4,'vocab_1'=8,'vocab_2'=2,'section'=4] {'vocab_1'}, dimensions={0}, use_global_device_ids=true | all-gather | bytes 258048 | tf_op jit(solution)/shard_map/all_gather | solution.py:37
  492.7 0.1 fusion.100
  492.8 0.1 concatenate.14
  492.9 1.8 all-gather.6
  494.8 0.1 concatenate.15
  494.8 11.4 %all-gather.7 = f32[4,28,256]{2,1,0:T(8,128)S(1)} all-gather(f32[1,28,256]{2,1,0:T(8,128)S(1)} %bitcast.1133), channel_id=5, replica_groups=mesh['vocab_0'=4,'vocab_1'=8,'vocab_2'=2,'section'=4] {'section'}, dimensions={0}, use_global_device_ids=true | all-gather | bytes 143360 | tf_op jit(solution)/shard_map/all_gather | solution.py:37
  506.2 0.0 copy-done
  506.2 1.3 multiply_reduce_fusion.2
  507.6 2.5 maximum_multiply_fusion
  (21 shorter events, 0.3 us)
Async XLA Ops:
  20.7 12.5 %copy-start.1 = (s32[4,256]{1,0:T(4,128)S(1)}, s32[4,256]{1,0:T(4,128)}, u32[]{:S(2)}) copy-start(s32[4,256]{1,0:T(4,128)} %param.8) | copy-start | bytes 12292
  20.7 377.2 %all-to-all-start.1 = ((bf16[64,4,4,8192]{3,2,1,0:T(4,128)(2,1)}), bf16[64,4,4,8192]{3,2,1,0:T(4,128)(2,1)}, u32[]{:S(2)}, u32[]{:S(2)}) async-start(bf16[64,4,4,8192]{3,2,1,0:T(4,128)(2,1)} %stack.15), calls=%async_computation.1 | async-start | bytes 33554432 | tf_op jit(solution)/shard_map/all_to_all | solution.py:110
  454.9 51.3 %copy-start = (s32[4,256]{1,0:T(4,128)S(1)}, s32[4,256]{1,0:T(4,128)}, u32[]{:S(2)}) copy-start(s32[4,256]{1,0:T(4,128)} %param.9) | copy-start | bytes 12292
